TPU v7x, 32 devices: a whole 2x2x4 slice. The times are simulated.
32 devices in a mesh: gx: 2 (over x), gy: 4 (over y, core), gz: 4 (over z).
Axes of the slice: x: 2, y: 2, z: 4, core: 2. Of those that a mesh axis runs over, the one named last changes fastest.
Arguments:
- state: float32 [53, 8, 16, 512], P(None, 'gx', 'gy', 'gz'), may hold values from -8 to 8
- diffusivity: float32 [53], replicated, may hold values from 0.01 to 0.08
- rates: float32 [53, 53], replicated, may hold values from -1.75 to 1.75
- inverse: float32 [53, 53, 8, 16, 512], P(None, None, 'gx', 'gy', 'gz'), may hold values from -3 to 5
- boundary: int32 [3], replicated, may hold values from 0 to 1, as said below
Outputs:
- new_state: float32 [53, 8, 16, 512], P(None, 'gx', 'gy', 'gz')
Inputs may be any that keep to these rules, and one draw needn't show every extreme that they name: `boundary`: 1 marks a dimension with periodic faces, 0 one with mirrored walls; at least one dimension has each kind.
All inputs are finite; a program needn't handle non-finite values.
Results may differ from a plain program's by a relative error of at most 0.00014.
Values sent between devices are 32-bit elements; how exact they have to be, the bound alone decides.
No kernel may reach another device: no remote copies, remote signals or barrier semaphores. Data moves between devices by JAX's collectives and lax.ppermute only.
A program may use at most 128 MiB of HBM per device.

v0:
```python
import jax
import jax.numpy as jnp
from jax import lax
from jax.sharding import PartitionSpec as P

NEWTON = 2


implicit_gamma = 0.2928932188134524
explicit_delta = -0.7071067811865475
rel_tol = 0.1
abs_tol = 0.05
drift_speed = 0.2


def with_halo(cells, sides, width):
    for axis, dim in sides:
        count = lax.axis_size(axis)
        head = lax.slice_in_dim(cells, 0, width, axis=dim)
        tail = lax.slice_in_dim(cells, cells.shape[dim] - width, cells.shape[dim], axis=dim)
        cells = jnp.concatenate(
            [
                lax.ppermute(tail, axis, [(i, (i + 1) % count) for i in range(count)]),
                cells,
                lax.ppermute(head, axis, [((i + 1) % count, i) for i in range(count)]),
            ],
            axis=dim,
        )
    return cells


def mirror_walls(extended, dim, flag, position, last_index):
    length = extended.shape[dim]
    low_ghost = lax.slice_in_dim(extended, 0, 2, axis=dim)
    high_ghost = lax.slice_in_dim(extended, length - 2, length, axis=dim)
    low_edge = jnp.flip(lax.slice_in_dim(extended, 2, 4, axis=dim), dim)
    high_edge = jnp.flip(lax.slice_in_dim(extended, length - 4, length - 2, axis=dim), dim)
    middle = lax.slice_in_dim(extended, 2, length - 2, axis=dim)
    walled = flag == 0
    low_part = jnp.where(walled & (position == 0), low_edge, low_ghost)
    high_part = jnp.where(walled & (position == last_index), high_edge, high_ghost)
    return jnp.concatenate([low_part, middle, high_part], axis=dim)


def stencil_terms(extended, dim):
    length = extended.shape[dim] - 4
    parts = [lax.slice_in_dim(extended, k, k + length, axis=dim) for k in range(5)]
    second = (-parts[0] + 16.0 * parts[1] - 30.0 * parts[2] + 16.0 * parts[3] - parts[4]) / 12.0
    return (second, parts[1])


def axis_terms(extended, dim, flag, axis_name):
    if axis_name == "gx":
        fixed = mirror_walls(extended, dim, flag, lax.axis_index("gx"), lax.axis_size("gx") - 1)
    elif axis_name == "gy":
        fixed = mirror_walls(extended, dim, flag, lax.axis_index("gy"), lax.axis_size("gy") - 1)
    else:
        fixed = mirror_walls(extended, dim, flag, lax.axis_index("gz"), lax.axis_size("gz") - 1)
    return stencil_terms(fixed, dim)


def transport(field, diffusivity, boundary):
    padded = with_halo(field, (("gx", 1), ("gy", 2), ("gz", 3)), 2)
    lap_x, below_x = axis_terms(padded[:, :, 2:-2, 2:-2], 1, boundary[0], "gx")
    lap_y, unused_y = axis_terms(padded[:, 2:-2, :, 2:-2], 2, boundary[1], "gy")
    lap_z, unused_z = axis_terms(padded[:, 2:-2, 2:-2, :], 3, boundary[2], "gz")
    return diffusivity[:, None, None, None] * (lap_x + lap_y + lap_z) - drift_speed * (
        field - below_x
    )


def chemistry(field, rates):
    return jnp.einsum("sj,jxyz->sxyz", rates, jnp.tanh(field), precision=lax.Precision.HIGHEST)


def global_total(local):
    partial_z = lax.psum(local, "gz")
    partial_y = lax.psum(partial_z, "gy")
    return lax.psum(partial_y, "gx")


def newton_solve(base, inverse, rates, weights):
    entries = base.shape[0] * base.shape[1] * base.shape[2] * base.shape[3]
    entries = entries * lax.axis_size("gx") * lax.axis_size("gy") * lax.axis_size("gz")
    guess = base
    for sweep in range(NEWTON):
        residual = guess - base - implicit_gamma * chemistry(guess, rates)
        update = jnp.einsum("sjxyz,jxyz->sxyz", inverse, residual, precision=lax.Precision.HIGHEST)
        local = jnp.sum(jnp.square(update * weights))
        norm_value = jnp.sqrt(global_total(local) / float(entries))
        guess = guess - update / jnp.maximum(norm_value, 1.0)
    return guess


def body(state, diffusivity, rates, inverse, boundary):
    weights = 1.0 / (rel_tol * jnp.abs(state) + abs_tol)
    first_rate = transport(state, diffusivity, boundary)
    section = newton_solve(state + implicit_gamma * first_rate, inverse, rates, weights)
    second_rate = transport(section, diffusivity, boundary)
    base = state + explicit_delta * first_rate + (1.0 - explicit_delta) * second_rate
    base = base + (1.0 - implicit_gamma) * chemistry(section, rates)
    return newton_solve(base, inverse, rates, weights)


def solution(mesh):
    in_specs = (P(None, "gx", "gy", "gz"), P(), P(), P(None, None, "gx", "gy", "gz"), P())
    out_specs = P(None, "gx", "gy", "gz")
    return jax.shard_map(body, mesh=mesh, in_specs=in_specs, out_specs=out_specs, check_vma=False)
```

profile of v0, /device:TPU:0, one launch (start us, length us, event | category | flops | bytes accessed | tf_op | source)
XLA Modules:
  0.0 227.1 jit_solution(8123236343109982432)
XLA Ops:
  0.0 1.2 copy.44
  1.2 3.0 %collective-permute-start.1 = (f32[53,2,4,128]{3,0,2,1:T(8,128)S(1)}, f32[53,2,4,128]{3,0,2,1:T(8,128)S(1)}, u32[]{:S(2)}, u32[]{:S(2)}) collective-permute-start(f32[53,2,4,128]{3,0,2,1:T(8,128)S(1)} %get-tuple-element.23), channel_id=1, source_target_pairs={{16,0},{0,16},{17,1},{1,17},{18,2},{2,18},{19,3},{3,19},{20,4},{4,... | collective-permute-start | bytes 651272 | tf_op jit(solution)/shard_map/ppermute | solution.py:25
  7.2 1.0 rev.44
  8.2 6.6 %collective-permute-done = f32[53,2,4,128]{3,0,2,1:T(8,128)S(1)} collective-permute-done((f32[53,2,4,128]{3,0,2,1:T(8,128)S(1)}, f32[53,2,4,128]{3,0,2,1:T(8,128)S(1)}, u32[]{:S(2)}, u32[]{:S(2)}) %collective-permute-start) | collective-permute-done | bytes 217120 | tf_op jit(solution)/shard_map/ppermute | solution.py:23
  15.0 0.7 reverse_select_fusion.2
  15.8 1.7 collective-permute-start.3
  17.6 0.8 fusion.114
  18.4 8.2 %collective-permute-done.2 = f32[53,8,2,128]{3,0,2,1:T(8,128)S(1)} collective-permute-done((f32[53,8,2,128]{3,0,2,1:T(8,128)S(1)}, f32[53,8,2,128]{3,0,2,1:T(8,128)S(1)}, u32[]{:S(2)}, u32[]{:S(2)}) %collective-permute-start.2) | collective-permute-done | bytes 434208 | tf_op jit(solution)/shard_map/ppermute | solution.py:23
  26.6 1.4 collective-permute-done.3
  27.9 0.8 copy-done.8
  28.8 1.9 fusion.107
  30.7 2.8 %copy.36 = f32[53,8,8,2]{0,2,3,1:T(8,128)} copy(f32[53,8,8,2]{3,0,2,1:T(8,128)} %get-tuple-element.7) | data formatting | bytes 54272 | tf_op jit(solution)/shard_map/slice | solution.py:20
  33.5 0.7 copy.40
  34.2 3.6 %collective-permute-start.5 = (f32[53,8,8,2]{0,2,3,1:T(8,128)S(1)}, f32[53,8,8,2]{0,2,3,1:T(8,128)S(1)}, u32[]{:S(2)}, u32[]{:S(2)}) collective-permute-start(f32[53,8,8,2]{0,2,3,1:T(8,128)S(1)} %copy.40), channel_id=1, source_target_pairs={{1,0},{2,1},{3,2},{0,3},{5,4},{6,5},{7,6},{4,7},{9,8},{10,9},{11,1... | collective-permute-start | bytes 81416 | tf_op jit(solution)/shard_map/ppermute | solution.py:25
  37.8 1.1 slice_select_fusion.3
  38.9 1.8 slice_select_fusion.2
  40.7 3.7 %collective-permute-done.4 = f32[53,8,8,2]{0,2,3,1:T(8,128)S(1)} collective-permute-done((f32[53,8,8,2]{0,2,3,1:T(8,128)}, f32[53,8,8,2]{0,2,3,1:T(8,128)S(1)}, u32[]{:S(2)}, u32[]{:S(2)}) %collective-permute-start.4) | collective-permute-done | bytes 27168 | tf_op jit(solution)/shard_map/ppermute | solution.py:23
  45.3 0.6 copy-done.10
  45.9 0.9 fusion.43
  46.8 0.8 fusion.13
  47.8 10.1 %multiply_reduce_fusion.3 = f32[4,4,128,53]{2,1,0,3:T(4,128)S(1)} fusion(f32[53,53,4,4,128]{4,3,2,1,0:T(4,128)} %param.8, f32[4,4,128,53]{2,1,0,3:T(4,128)S(1)} %copy.85), kind=kLoop, calls=%fused_computation.3 | loop fusion | flops 11397120 | bytes 23879680
  57.8 0.9 fusion.92
  58.8 9.1 %psum.84 = f32[]{:T(128)} all-reduce(f32[]{:T(128)} %fusion.92), channel_id=1, replica_groups=mesh['gx'=2,'gy'=4,'gz'=4] {'gz'}, use_global_device_ids=true, to_apply=%region_1.2 | all-reduce | flops 1 | bytes 8 | tf_op jit(solution)/shard_map/psum | solution.py:77
  67.9 6.6 %psum.85 = f32[]{:T(128)} all-reduce(f32[]{:T(128)} %psum.84), channel_id=1, replica_groups=mesh['gx'=2,'gy'=4,'gz'=4] {'gy'}, use_global_device_ids=true, to_apply=%region_2.3 | all-reduce | flops 1 | bytes 8 | tf_op jit(solution)/shard_map/psum | solution.py:78
  74.5 5.5 %psum.86 = f32[]{:T(128)} all-reduce(f32[]{:T(128)} %psum.85), channel_id=1, replica_groups=mesh['gx'=2,'gy'=4,'gz'=4] {'gx'}, use_global_device_ids=true, to_apply=%region_3.4 | all-reduce | flops 1 | bytes 8 | tf_op jit(solution)/shard_map/psum | solution.py:79
  80.8 1.1 fusion.10
  82.0 10.1 %multiply_reduce_fusion.2 = f32[4,4,128,53]{2,1,0,3:T(4,128)S(1)} fusion(f32[53,53,4,4,128]{4,3,2,1,0:T(4,128)} %param.8, f32[4,4,128,53]{2,1,0,3:T(4,128)S(1)} %copy.86), kind=kLoop, calls=%fused_computation.2 | loop fusion | flops 11397120 | bytes 23879680
  92.0 0.9 fusion.89
  93.0 10.6 %psum.87 = f32[]{:T(128)} all-reduce(f32[]{:T(128)} %fusion.89), channel_id=1, replica_groups=mesh['gx'=2,'gy'=4,'gz'=4] {'gz'}, use_global_device_ids=true, to_apply=%region_5.6 | all-reduce | flops 1 | bytes 8 | tf_op jit(solution)/shard_map/psum | solution.py:77
  103.5 6.4 %psum.88 = f32[]{:T(128)} all-reduce(f32[]{:T(128)} %psum.87), channel_id=1, replica_groups=mesh['gx'=2,'gy'=4,'gz'=4] {'gy'}, use_global_device_ids=true, to_apply=%region_6.7 | all-reduce | flops 1 | bytes 8 | tf_op jit(solution)/shard_map/psum | solution.py:78
  109.9 5.5 %psum.89 = f32[]{:T(128)} all-reduce(f32[]{:T(128)} %psum.88), channel_id=1, replica_groups=mesh['gx'=2,'gy'=4,'gz'=4] {'gx'}, use_global_device_ids=true, to_apply=%region_7.8 | all-reduce | flops 1 | bytes 8 | tf_op jit(solution)/shard_map/psum | solution.py:79
  116.8 1.6 collective-permute-start.6
  118.9 1.0 rev.49
  119.8 1.0 rev.50
  120.8 0.7 fusion.111
  121.5 3.8 %collective-permute-done.6 = f32[53,2,4,128]{3,0,2,1:T(8,128)S(1)} collective-permute-done((f32[53,2,4,128]{3,0,2,1:T(8,128)S(1)}, f32[53,2,4,128]{3,0,2,1:T(8,128)S(1)}, u32[]{:S(2)}, u32[]{:S(2)}) %collective-permute-start.6) | collective-permute-done | bytes 217120 | tf_op jit(solution)/shard_map/ppermute | solution.py:23
  125.3 3.1 %collective-permute-done.7 = f32[53,2,4,128]{3,0,2,1:T(8,128)S(1)} collective-permute-done((f32[53,2,4,128]{3,0,2,1:T(8,128)S(1)}, f32[53,2,4,128]{3,0,2,1:T(8,128)S(1)}, u32[]{:S(2)}, u32[]{:S(2)}) %collective-permute-start.7) | collective-permute-done | bytes 217120 | tf_op jit(solution)/shard_map/ppermute | solution.py:25
  128.7 1.7 collective-permute-start.9
  130.4 0.7 reverse_select_fusion.1
  131.1 0.7 reverse_select_fusion
  131.8 7.7 %collective-permute-done.8 = f32[53,8,2,128]{3,0,2,1:T(8,128)S(1)} collective-permute-done((f32[53,8,2,128]{3,0,2,1:T(8,128)S(1)}, f32[53,8,2,128]{3,0,2,1:T(8,128)S(1)}, u32[]{:S(2)}, u32[]{:S(2)}) %collective-permute-start.8) | collective-permute-done | bytes 434208 | tf_op jit(solution)/shard_map/ppermute | solution.py:23
  139.6 1.1 collective-permute-done.9
  140.6 0.8 copy-done.6
  141.6 1.9 fusion.106
  143.4 2.8 %copy.47 = f32[53,8,8,2]{0,2,3,1:T(8,128)} copy(f32[53,8,8,2]{3,0,2,1:T(8,128)} %get-tuple-element.5) | data formatting | bytes 54272 | tf_op jit(solution)/shard_map/slice | solution.py:20
  146.2 0.7 copy.49
  147.4 1.6 collective-permute-start.10
  149.0 1.8 slice_select_fusion.1
  150.8 1.7 slice_select_fusion
  152.4 1.4 collective-permute-done.10
  155.7 1.3 fusion.7
  156.9 0.6 fusion.5
  157.7 10.1 %multiply_reduce_fusion.1 = f32[4,4,128,53]{2,1,0,3:T(4,128)S(1)} fusion(f32[53,53,4,4,128]{4,3,2,1,0:T(4,128)} %param.8, f32[4,4,128,53]{2,1,0,3:T(4,128)S(1)} %copy.87), kind=kLoop, calls=%fused_computation.1 | loop fusion | flops 11397120 | bytes 23879680
  167.8 0.9 fusion.86
  168.7 9.8 %psum.90 = f32[]{:T(128)} all-reduce(f32[]{:T(128)} %fusion.86), channel_id=1, replica_groups=mesh['gx'=2,'gy'=4,'gz'=4] {'gz'}, use_global_device_ids=true, to_apply=%region_9.10 | all-reduce | flops 1 | bytes 8 | tf_op jit(solution)/shard_map/psum | solution.py:77
  178.5 6.7 %psum.91 = f32[]{:T(128)} all-reduce(f32[]{:T(128)} %psum.90), channel_id=1, replica_groups=mesh['gx'=2,'gy'=4,'gz'=4] {'gy'}, use_global_device_ids=true, to_apply=%region_10.11 | all-reduce | flops 1 | bytes 8 | tf_op jit(solution)/shard_map/psum | solution.py:78
  185.2 5.5 %psum.92 = f32[]{:T(128)} all-reduce(f32[]{:T(128)} %psum.91), channel_id=1, replica_groups=mesh['gx'=2,'gy'=4,'gz'=4] {'gx'}, use_global_device_ids=true, to_apply=%region_11.12 | all-reduce | flops 1 | bytes 8 | tf_op jit(solution)/shard_map/psum | solution.py:79
  191.4 0.8 fusion.2
  192.4 10.1 %multiply_reduce_fusion = f32[4,4,128,53]{2,1,0,3:T(4,128)S(1)} fusion(f32[53,53,4,4,128]{4,3,2,1,0:T(4,128)} %param.8, f32[4,4,128,53]{2,1,0,3:T(4,128)S(1)} %copy.88), kind=kLoop, calls=%fused_computation | loop fusion | flops 11397120 | bytes 23879680
  202.4 0.9 fusion.83
  203.4 10.0 %psum.93 = f32[]{:T(128)} all-reduce(f32[]{:T(128)} %fusion.83), channel_id=1, replica_groups=mesh['gx'=2,'gy'=4,'gz'=4] {'gz'}, use_global_device_ids=true, to_apply=%region_13.14 | all-reduce | flops 1 | bytes 8 | tf_op jit(solution)/shard_map/psum | solution.py:77
  213.3 6.4 %psum.94 = f32[]{:T(128)} all-reduce(f32[]{:T(128)} %psum.93), channel_id=1, replica_groups=mesh['gx'=2,'gy'=4,'gz'=4] {'gy'}, use_global_device_ids=true, to_apply=%region_14.15 | all-reduce | flops 1 | bytes 8 | tf_op jit(solution)/shard_map/psum | solution.py:78
  219.7 5.5 %psum.95 = f32[]{:T(128)} all-reduce(f32[]{:T(128)} %psum.94), channel_id=1, replica_groups=mesh['gx'=2,'gy'=4,'gz'=4] {'gx'}, use_global_device_ids=true, to_apply=%region_15.16 | all-reduce | flops 1 | bytes 8 | tf_op jit(solution)/shard_map/psum | solution.py:79
  226.2 0.9 copy.51
  (71 shorter events, 6.8 us)
Async XLA Ops:
  0.0 46.8 %copy-start = (f32[53,53]{1,0:T(8,128)S(1)}, f32[53,53]{1,0:T(8,128)}, u32[]{:S(2)}) copy-start(f32[53,53]{1,0:T(8,128)} %param.7) | copy-start | bytes 33712
  0.0 4.3 %copy-start.15 = (s32[3]{0:T(128)S(1)}, s32[3]{0:T(128)}, u32[]{:S(2)}) copy-start(s32[3]{0:T(128)} %param.9) | copy-start | bytes 40
  1.2 13.8 %collective-permute-start.1 = (f32[53,2,4,128]{3,0,2,1:T(8,128)S(1)}, f32[53,2,4,128]{3,0,2,1:T(8,128)S(1)}, u32[]{:S(2)}, u32[]{:S(2)}) collective-permute-start(f32[53,2,4,128]{3,0,2,1:T(8,128)S(1)} %get-tuple-element.23), channel_id=1, source_target_pairs={{16,0},{0,16},{17,1},{1,17},{18,2},{2,18},{19,3},{3,19},{20,4},{4,... | collective-permute-start | bytes 651272 | tf_op jit(solution)/shard_map/ppermute | solution.py:25
  4.3 10.5 %collective-permute-start = (f32[53,2,4,128]{3,0,2,1:T(8,128)S(1)}, f32[53,2,4,128]{3,0,2,1:T(8,128)S(1)}, u32[]{:S(2)}, u32[]{:S(2)}) collective-permute-start(f32[53,2,4,128]{3,0,2,1:T(8,128)S(1)} %get-tuple-element.24), channel_id=1, source_target_pairs={{0,16},{16,0},{1,17},{17,1},{2,18},{18,2},{3,19},{19,3},{4,20},{20... | collective-permute-start | bytes 651272 | tf_op jit(solution)/shard_map/ppermute | solution.py:23
  7.1 7.8 %copy-start.1 = (f32[53,4,4,128]{3,2,1,0:T(4,128)S(1)}, f32[53,4,4,128]{3,2,1,0:T(4,128)}, u32[]{:S(2)}) copy-start(f32[53,4,4,128]{3,2,1,0:T(4,128)} %param.5) | copy-start | bytes 1302532
  14.8 2.8 %copy-start.16 = (f32[53]{0:T(128)S(1)}, f32[53]{0:T(128)}, u32[]{:S(2)}) copy-start(f32[53]{0:T(128)} %param.6) | copy-start | bytes 640
  15.8 10.8 %collective-permute-start.2 = (f32[53,8,2,128]{3,0,2,1:T(8,128)S(1)}, f32[53,8,2,128]{3,0,2,1:T(8,128)S(1)}, u32[]{:S(2)}, u32[]{:S(2)}) collective-permute-start(f32[53,8,2,128]{3,0,2,1:T(8,128)S(1)} %get-tuple-element.11), channel_id=1, source_target_pairs={{0,4},{4,8},{8,12},{12,0},{1,5},{5,9},{9,13},{13,1},{2,6},{6,10},{... | collective-permute-start | bytes 1302536 | tf_op jit(solution)/shard_map/ppermute | solution.py:23
  15.8 12.1 %collective-permute-start.3 = (f32[53,8,2,128]{3,0,2,1:T(8,128)S(1)}, f32[53,8,2,128]{3,0,2,1:T(8,128)S(1)}, u32[]{:S(2)}, u32[]{:S(2)}) collective-permute-start(f32[53,8,2,128]{3,0,2,1:T(8,128)S(1)} %get-tuple-element.12), channel_id=1, source_target_pairs={{4,0},{8,4},{12,8},{0,12},{5,1},{9,5},{13,9},{1,13},{6,2},{10,6},{... | collective-permute-start | bytes 1302536 | tf_op jit(solution)/shard_map/ppermute | solution.py:25
  26.6 1.4 copy-start.7
  27.9 0.8 copy-start.8
  34.2 10.7 %copy-start.2 = (f32[53,4,4,2]{3,0,2,1:T(8,128)S(1)}, f32[53,4,4,2]{3,0,2,1:T(8,128)}, u32[]{:S(2)}) copy-start(f32[53,4,4,2]{3,0,2,1:T(8,128)} %rev.44) | copy-start | bytes 20356
  34.2 10.4 %collective-permute-start.5 = (f32[53,8,8,2]{0,2,3,1:T(8,128)S(1)}, f32[53,8,8,2]{0,2,3,1:T(8,128)S(1)}, u32[]{:S(2)}, u32[]{:S(2)}) collective-permute-start(f32[53,8,8,2]{0,2,3,1:T(8,128)S(1)} %copy.40), channel_id=1, source_target_pairs={{1,0},{2,1},{3,2},{0,3},{5,4},{6,5},{7,6},{4,7},{9,8},{10,9},{11,1... | collective-permute-start | bytes 81416 | tf_op jit(solution)/shard_map/ppermute | solution.py:25
  37.8 6.5 %collective-permute-start.4 = (f32[53,8,8,2]{0,2,3,1:T(8,128)}, f32[53,8,8,2]{0,2,3,1:T(8,128)S(1)}, u32[]{:S(2)}, u32[]{:S(2)}) collective-permute-start(f32[53,8,8,2]{0,2,3,1:T(8,128)} %copy.36), channel_id=1, source_target_pairs={{0,1},{1,2},{2,3},{3,0},{4,5},{5,6},{6,7},{7,4},{8,9},{9,10},{10,1... | collective-permute-start | bytes 81416 | tf_op jit(solution)/shard_map/ppermute | solution.py:23
  44.4 0.9 copy-start.9
  44.9 1.0 copy-start.10
  116.8 8.5 %collective-permute-start.6 = (f32[53,2,4,128]{3,0,2,1:T(8,128)S(1)}, f32[53,2,4,128]{3,0,2,1:T(8,128)S(1)}, u32[]{:S(2)}, u32[]{:S(2)}) collective-permute-start(f32[53,2,4,128]{3,0,2,1:T(8,128)S(1)} %get-tuple-element.17), channel_id=1, source_target_pairs={{0,16},{16,0},{1,17},{17,1},{2,18},{18,2},{3,19},{19,3},{4,20},{20... | collective-permute-start | bytes 651272 | tf_op jit(solution)/shard_map/ppermute | solution.py:23
  118.4 10.1 %collective-permute-start.7 = (f32[53,2,4,128]{3,0,2,1:T(8,128)S(1)}, f32[53,2,4,128]{3,0,2,1:T(8,128)S(1)}, u32[]{:S(2)}, u32[]{:S(2)}) collective-permute-start(f32[53,2,4,128]{3,0,2,1:T(8,128)S(1)} %get-tuple-element.18), channel_id=1, source_target_pairs={{16,0},{0,16},{17,1},{1,17},{18,2},{2,18},{19,3},{3,19},{20,4},{4,... | collective-permute-start | bytes 651272 | tf_op jit(solution)/shard_map/ppermute | solution.py:25
  128.6 10.9 %collective-permute-start.8 = (f32[53,8,2,128]{3,0,2,1:T(8,128)S(1)}, f32[53,8,2,128]{3,0,2,1:T(8,128)S(1)}, u32[]{:S(2)}, u32[]{:S(2)}) collective-permute-start(f32[53,8,2,128]{3,0,2,1:T(8,128)S(1)} %get-tuple-element.9), channel_id=1, source_target_pairs={{0,4},{4,8},{8,12},{12,0},{1,5},{5,9},{9,13},{13,1},{2,6},{6,10},{... | collective-permute-start | bytes 1302536 | tf_op jit(solution)/shard_map/ppermute | solution.py:23
  128.7 12.0 %collective-permute-start.9 = (f32[53,8,2,128]{3,0,2,1:T(8,128)S(1)}, f32[53,8,2,128]{3,0,2,1:T(8,128)S(1)}, u32[]{:S(2)}, u32[]{:S(2)}) collective-permute-start(f32[53,8,2,128]{3,0,2,1:T(8,128)S(1)} %get-tuple-element.10), channel_id=1, source_target_pairs={{4,0},{8,4},{12,8},{0,12},{5,1},{9,5},{13,9},{1,13},{6,2},{10,6},{... | collective-permute-start | bytes 1302536 | tf_op jit(solution)/shard_map/ppermute | solution.py:25
  139.6 1.1 copy-start.5
  140.6 0.8 copy-start.6
  146.9 7.5 %copy-start.4 = (f32[53,4,4,2]{3,0,2,1:T(8,128)S(1)}, f32[53,4,4,2]{3,0,2,1:T(8,128)}, u32[]{:S(2)}) copy-start(f32[53,4,4,2]{3,0,2,1:T(8,128)} %rev.49) | copy-start | bytes 20356
  146.9 7.3 %collective-permute-start.11 = (f32[53,8,8,2]{0,2,3,1:T(8,128)S(1)}, f32[53,8,8,2]{0,2,3,1:T(8,128)S(1)}, u32[]{:S(2)}, u32[]{:S(2)}) collective-permute-start(f32[53,8,8,2]{0,2,3,1:T(8,128)S(1)} %copy.49), channel_id=1, source_target_pairs={{1,0},{2,1},{3,2},{0,3},{5,4},{6,5},{7,6},{4,7},{9,8},{10,9},{11,1... | collective-permute-start | bytes 81416 | tf_op jit(solution)/shard_map/ppermute | solution.py:25
  147.4 6.5 %collective-permute-start.10 = (f32[53,8,8,2]{0,2,3,1:T(8,128)}, f32[53,8,8,2]{0,2,3,1:T(8,128)S(1)}, u32[]{:S(2)}, u32[]{:S(2)}) collective-permute-start(f32[53,8,8,2]{0,2,3,1:T(8,128)} %copy.47), channel_id=1, source_target_pairs={{0,1},{1,2},{2,3},{3,0},{4,5},{5,6},{6,7},{7,4},{8,9},{9,10},{10,1... | collective-permute-start | bytes 81416 | tf_op jit(solution)/shard_map/ppermute | solution.py:23
  149.0 5.6 %copy-start.3 = (f32[53,4,4,2]{3,0,2,1:T(8,128)S(1)}, f32[53,4,4,2]{3,0,2,1:T(8,128)}, u32[]{:S(2)}) copy-start(f32[53,4,4,2]{3,0,2,1:T(8,128)} %rev.50) | copy-start | bytes 20356
  153.9 0.9 copy-start.11
  154.5 1.0 copy-start.12
  154.5 1.1 copy-start.13
  154.5 1.2 copy-start.14
where the time goes:
time: 228 us; the launch traced here: 227 us
  blocking collectives  87.7 us (38%)
  other arithmetic  54.5 us (24%)
  waiting for transfers between devices  36.9 us (16%)
  local copies, waits for them, and re-layouts  23.7 us (10%)
  starting transfers between devices  14.5 us (6%)
  between operations  5.08 us (2%)
  matrix products  4.64 us (2%)
    unnamed x4, other arithmetic  40.2 us
    psum x4, blocking collectives, global_total(): partial_z = lax.psum(local, 'gz')  39.5 us
    ppermute x6, waiting for transfers between devices, with_halo(): lax.ppermute(tail, axis, [(i, (i + 1) % count) for i in range(count)])  31.4 us
    psum x4, blocking collectives, global_total(): partial_y = lax.psum(partial_z, 'gy')  26.1 us
    psum x4, blocking collectives, global_total(): return lax.psum(partial_y, 'gx')  22.2 us
    ppermute x6, starting transfers between devices, with_halo(): lax.ppermute(head, axis, [((i + 1) % count, i) for i in range(count)])  11.2 us
    slice x7, local copies, waits for them, and re-layouts, with_halo(): lax.slice_in_dim(cells, cells.shape[dim] - width, cells.shape[dim], axis=...  9.46 us
    ppermute x6, waiting for transfers between devices, with_halo(): lax.ppermute(head, axis, [((i + 1) % count, i) for i in range(count)])  5.58 us
  transfers between devices with their start and end apart: 12, of which 9 were waited for; matrix products, arithmetic and copies ran while one was open for 6% of the time, Pallas kernels for 0%

commit v1 on v0

v1 whole, which is shorter than its diff:
```python
import functools

import jax
import jax.numpy as jnp
from jax import lax
from jax.experimental import pallas as pl
from jax.experimental.pallas import tpu as pltpu
from jax.sharding import PartitionSpec as P

NEWTON = 2
AXES = ("gx", "gy", "gz")
SUB = 8

implicit_gamma = 0.2928932188134524
explicit_delta = -0.7071067811865475
rel_tol = 0.1
abs_tol = 0.05
drift_speed = 0.2

VMEM = pl.BlockSpec(memory_space=pltpu.VMEM)
SMEM = pl.BlockSpec(memory_space=pltpu.SMEM)
f32 = jnp.float32


def iota(dim, lanes):
    return lax.broadcasted_iota(jnp.int32, (SUB, lanes), dim)


def turn(value, shift, axis):
    size = value.shape[axis]
    return pltpu.roll(value, shift % size, axis)


def groups_of(rows):
    return rows // SUB


def pack_faces(load, species, groups, lanes, tail_y, head_y, tail_z, head_z):
    row = iota(0, lanes) % 4
    lane = iota(1, lanes)
    per = lanes // 2
    packs = tail_z.shape[0] // SUB
    tails = [jnp.zeros((SUB, lanes), f32) for _ in range(packs)]
    heads = [jnp.zeros((SUB, lanes), f32) for _ in range(packs)]
    for s in range(species):
        v = [load(s, g) for g in range(groups)]
        for k in range(groups // 2):
            a, b = v[2 * k], v[2 * k + 1]
            tail_y[s, k * SUB : (k + 1) * SUB, :] = jnp.where(row >= 2, a, turn(b, -2, 0))
            head_y[s, k * SUB : (k + 1) * SUB, :] = jnp.where(row < 2, a, turn(b, 2, 0))
        for g in range(groups):
            p, q = divmod(s * groups + g, per)
            here = lane // 2 == q
            tails[p] = jnp.where(here, turn(v[g], 2 * q + 2, 1), tails[p])
            heads[p] = jnp.where(here, turn(v[g], 2 * q, 1), heads[p])
    for p in range(packs):
        tail_z[p * SUB : (p + 1) * SUB, :] = tails[p]
        head_z[p * SUB : (p + 1) * SUB, :] = heads[p]


def wall_flags(kinds):
    out = []
    for i, axis in enumerate(AXES):
        walled = kinds[i] == 0
        here, last = lax.axis_index(axis), lax.axis_size(axis) - 1
        out.append((walled & (here == 0), walled & (here == last)))
    return out


def transport(load, store, species, groups, lanes, faces, diffusivity, kinds):
    load_low, load_high, tail_y, head_y, tail_z, head_z, edges = faces
    (wall_x0, wall_x1), (wall_y0, wall_y1), (wall_z0, wall_z1) = wall_flags(kinds)
    row = iota(0, lanes) % 4
    lane = iota(1, lanes)
    low_half = iota(0, lanes) < 4
    zero = jnp.zeros((SUB, lanes), f32)

    def along(pos, length, wall0, wall1):
        w0 = jnp.where(wall0, 1.0, 0.0).astype(f32)
        w1 = jnp.where(wall1, 1.0, 0.0).astype(f32)
        at = lambda k: pos == k
        centre = jnp.where(at(0), 16.0 * w0, jnp.where(at(length - 1), 16.0 * w1, 0.0)) - 30.0
        up1 = jnp.where(at(0), 0.0, 16.0) - jnp.where(at(1), w0, 0.0) - jnp.where(at(length - 1), w1, 0.0)
        dn1 = jnp.where(at(length - 1), 0.0, 16.0) - jnp.where(at(0), w0, 0.0) - jnp.where(at(length - 2), w1, 0.0)
        up2 = jnp.where(pos < 2, 0.0, -1.0)
        dn2 = jnp.where(pos >= length - 2, 0.0, -1.0)
        return centre, up1, dn1, up2, dn2, 1.0 - w0, 1.0 - w1

    cy, uy1, dy1, uy2, dy2, keep_y0, keep_y1 = along(row, 4, wall_y0, wall_y1)
    cz, uz1, dz1, uz2, dz2, keep_z0, keep_z1 = along(lane, lanes, wall_z0, wall_z1)
    centre = cy + cz - 30.0
    a01 = jnp.where(row < 2, -keep_y0, 0.0)
    a0 = jnp.where(row == 0, 16.0 * keep_y0, 0.0)
    b23 = jnp.where(row >= 2, -keep_y1, 0.0)
    b3 = jnp.where(row == 3, 16.0 * keep_y1, 0.0)
    edge = (lane < 2) | (lane >= lanes - 2)
    per = lanes // 2
    packs = tail_z.shape[0] // SUB
    even = lane % 2 == 0
    first = lane % 4 < 2
    for p in range(packs):
        span = slice(p * SUB, (p + 1) * SUB)
        low, high = tail_z[span, :], head_z[span, :]
        low = (jnp.where(even, 16.0 * turn(low, -1, 1), 0.0) - low) * keep_z0
        high = (jnp.where(even, 0.0, 16.0 * turn(high, 1, 1)) - high) * keep_z1
        high = turn(high, -2, 1)
        edges[0, span, :] = jnp.where(first, low, high)
        edges[1, span, :] = jnp.where(first, high, low)

    for s in range(species):
        v = [load(s, g) for g in range(groups)]
        half = [turn(u, 4, 0) for u in v]
        ghost_low = jnp.where(wall_x0, half[0], load_low(s))
        ghost_high = jnp.where(wall_x1, half[-1], load_high(s))
        chain = [ghost_low] + v + [ghost_high]
        halves = [turn(ghost_low, 4, 0)] + half + [turn(ghost_high, 4, 0)]
        scale = diffusivity[s] * (1.0 / 12.0)
        for g in range(groups):
            u = v[g]
            below = jnp.where(low_half, halves[g], halves[g + 1])
            above = jnp.where(low_half, halves[g + 1], halves[g + 2])
            total = centre * u + 16.0 * (below + above) - (chain[g] + chain[g + 2])
            total = total + uy1 * turn(u, 1, 0) + dy1 * turn(u, -1, 0)
            total = total + uy2 * turn(u, 2, 0) + dy2 * turn(u, -2, 0)
            span = slice(g // 2 * SUB, (g // 2 + 1) * SUB)
            t, h = tail_y[s, span, :], head_y[s, span, :]
            if g % 2 == 0:
                total = total + a01 * turn(t, -2, 0) + a0 * turn(t, -3, 0)
                total = total + b23 * turn(h, 2, 0) + b3 * turn(h, 3, 0)
            else:
                total = total + a01 * t + a0 * turn(t, -1, 0)
                total = total + b23 * h + b3 * turn(h, 1, 0)
            total = total + uz1 * turn(u, 1, 1) + dz1 * turn(u, -1, 1)
            total = total + uz2 * turn(u, 2, 1) + dz2 * turn(u, -2, 1)
            p, q = divmod(s * groups + g, per)
            ends = turn(edges[q % 2, p * SUB : (p + 1) * SUB, :], -2 * q, 1)
            total = total + jnp.where(edge, ends, zero)
            store(s, g, u, scale * total - drift_speed * (u - below))


def chemistry(acts, rates, out, rows, lanes):
    padded = rates.shape[0]
    cols = [acts[pl.ds(r, padded, stride=rows), :] for r in range(rows)]
    made = jnp.dot(
        rates[...], jnp.concatenate(cols, axis=1), precision=lax.Precision.HIGHEST, preferred_element_type=f32
    )
    for r in range(rows):
        out[pl.ds(r, padded, stride=rows), :] = made[:, r * lanes : (r + 1) * lanes]


def blank_tail(acts, species, rows, lanes):
    padded = acts.shape[0] // rows
    if padded > species:
        acts[species * rows :, :] = jnp.zeros(((padded - species) * rows, lanes), f32)


def matvec(inverse, residual, weights, update, partial, species, rows, lanes, block=4):
    def some(first, count, squares):
        acc = [None] * count
        for j in range(species):
            g = residual[j * rows : (j + 1) * rows, :]
            for i in range(count):
                term = inverse[first + i, j] * g
                acc[i] = term if acc[i] is None else acc[i] + term
        for i in range(count):
            update[first + i] = acc[i]
            scaled = acc[i] * weights[first + i]
            squares = squares + scaled * scaled
        return squares

    squares = jnp.zeros((rows, lanes), f32)
    whole = species // block
    squares = lax.fori_loop(0, whole, lambda k, c: some(k * block, block, c), squares)
    if species % block:
        squares = some(whole * block, species % block, squares)
    partial[...] = jnp.broadcast_to(jnp.sum(squares, axis=0, keepdims=True), partial.shape)


def damping(parts, entries):
    total = jnp.sum(parts[...], axis=(0, 1), keepdims=True)
    return 1.0 / jnp.maximum(jnp.sqrt(total * (1.0 / entries)), 1.0)


def pack_kernel(state, tail_y, head_y, tail_z, head_z):
    species, rows, lanes = state.shape
    load = lambda s, g: state[s, g * SUB : (g + 1) * SUB, :]
    pack_faces(load, species, groups_of(rows), lanes, tail_y, head_y, tail_z, head_z)


def face_loads(refs, lanes):
    if len(refs) == 1:
        block = refs[0]
        rows = block.shape[1]
        return (lambda s: block[s, rows - SUB :, :]), (lambda s: block[s, :SUB, :])
    low, high = refs
    return (lambda s: low[s]), (lambda s: high[s])


def first_kernel(x_faces, state, *refs):
    xs, refs = refs[:x_faces], refs[x_faces:]
    tail_y, head_y, tail_z, head_z, diffusivity, kinds, rates, inverse = refs[:8]
    rate0, base, weights, update, partial, acts, made, edges = refs[8:]
    species, rows, lanes = state.shape
    groups = groups_of(rows)
    low, high = face_loads(xs, lanes)

    def store(s, g, u, e):
        span = slice(g * SUB, (g + 1) * SUB)
        rate0[s, span, :] = e
        b = u + implicit_gamma * e
        base[s, span, :] = b
        acts[s * rows + g * SUB : s * rows + (g + 1) * SUB, :] = jnp.tanh(b)
        weights[s, span, :] = 1.0 / (rel_tol * jnp.abs(u) + abs_tol)

    load = lambda s, g: state[s, g * SUB : (g + 1) * SUB, :]
    blank_tail(acts, species, rows, lanes)
    transport(load, store, species, groups, lanes, (low, high, tail_y, head_y, tail_z, head_z, edges), diffusivity, kinds)
    chemistry(acts, rates, made, rows, lanes)
    made[...] = made[...] * -implicit_gamma
    matvec(inverse, made, weights, update, partial, species, rows, lanes)


def next_kernel(entries, parts, base, update, weights, rates, inverse, guess, second, partial, acts, made):
    species, rows, lanes = base.shape
    scale = damping(parts, entries)
    blank_tail(acts, species, rows, lanes)
    for s in range(species):
        z = base[s] - update[s] * scale
        guess[s] = z
        acts[s * rows : (s + 1) * rows, :] = jnp.tanh(z)
    chemistry(acts, rates, made, rows, lanes)
    for s in range(species):
        span = slice(s * rows, (s + 1) * rows)
        made[span, :] = (guess[s] - base[s]) - implicit_gamma * made[span, :]
    matvec(inverse, made, weights, second, partial, species, rows, lanes)


def section_kernel(entries, parts, guess, update, section, tail_y, head_y, tail_z, head_z):
    species, rows, lanes = guess.shape
    scale = damping(parts, entries)

    def load(s, g):
        span = slice(g * SUB, (g + 1) * SUB)
        z = guess[s, span, :] - update[s, span, :] * scale
        section[s, span, :] = z
        return z

    pack_faces(load, species, groups_of(rows), lanes, tail_y, head_y, tail_z, head_z)


def second_kernel(x_faces, section, *refs):
    xs, refs = refs[:x_faces], refs[x_faces:]
    tail_y, head_y, tail_z, head_z, diffusivity, kinds, rates, inverse, state, rate0, weights = refs[:11]
    base, update, partial, acts, made, edges = refs[11:]
    species, rows, lanes = state.shape
    groups = groups_of(rows)
    low, high = face_loads(xs, lanes)

    def store(s, g, u, e):
        span = slice(g * SUB, (g + 1) * SUB)
        mixed = state[s, span, :] + explicit_delta * rate0[s, span, :] + (1.0 - explicit_delta) * e
        base[s, span, :] = mixed
        acts[s * rows + g * SUB : s * rows + (g + 1) * SUB, :] = jnp.tanh(u)

    load = lambda s, g: section[s, g * SUB : (g + 1) * SUB, :]
    blank_tail(acts, species, rows, lanes)
    transport(load, store, species, groups, lanes, (low, high, tail_y, head_y, tail_z, head_z, edges), diffusivity, kinds)
    chemistry(acts, rates, made, rows, lanes)
    for s in range(species):
        span = slice(s * rows, (s + 1) * rows)
        b = base[s] + (1.0 - implicit_gamma) * made[span, :]
        base[s] = b
        acts[span, :] = jnp.tanh(b)
    chemistry(acts, rates, made, rows, lanes)
    made[...] = made[...] * -implicit_gamma
    matvec(inverse, made, weights, update, partial, species, rows, lanes)


def last_kernel(entries, parts, guess, update, out):
    scale = damping(parts, entries)
    for s in range(guess.shape[0]):
        out[s] = guess[s] - update[s] * scale


def shaped(*dims):
    return jax.ShapeDtypeStruct(dims, f32)


def call(kernel, outs, specs, args, scratch=(), cost=0, limit=8 << 20, name=None):
    return pl.pallas_call(
        kernel,
        out_shape=outs,
        in_specs=specs,
        out_specs=jax.tree.map(lambda _: VMEM, outs),
        scratch_shapes=scratch,
        compiler_params=pltpu.CompilerParams(vmem_limit_bytes=limit),
        cost_estimate=pl.CostEstimate(flops=cost, bytes_accessed=cost, transcendentals=0),
        name=name,
    )(*args)


def ring(axis, step):
    count = lax.axis_size(axis)
    return [(i, (i + step) % count) for i in range(count)]


def exchange(block, tail_y, head_y, tail_z, head_z):
    rows = block.shape[1]
    if lax.axis_size("gx") == 2 and rows == 2 * SUB:
        xs = [lax.ppermute(block, "gx", ring("gx", 1))]
    else:
        low = lax.ppermute(block[:, rows - SUB :, :], "gx", ring("gx", 1))
        xs = [low, lax.ppermute(block[:, :SUB, :], "gx", ring("gx", -1))]
    ys = [lax.ppermute(tail_y, "gy", ring("gy", 1)), lax.ppermute(head_y, "gy", ring("gy", -1))]
    zs = [lax.ppermute(tail_z, "gz", ring("gz", 1)), lax.ppermute(head_z, "gz", ring("gz", -1))]
    return xs, ys + zs


def body(state, diffusivity, rates, inverse, boundary):
    species, nx, ny, lanes = state.shape
    rows = nx * ny
    groups = groups_of(rows)
    assert ny * 2 == SUB and groups % 2 == 0 and lanes == 128
    devices = lax.axis_size("gx") * lax.axis_size("gy") * lax.axis_size("gz")
    entries = float(species * rows * lanes * devices)
    padded = -(-species // SUB) * SUB
    packs = -(-species * groups * 2 // lanes)
    block = shaped(species, rows, lanes)
    faces = [shaped(species, groups // 2 * SUB, lanes)] * 2 + [shaped(packs * SUB, lanes)] * 2
    partial = shaped(devices, lanes)
    flat = pltpu.VMEM((padded * rows, lanes), f32)
    edges = pltpu.VMEM((2, packs * SUB, lanes), f32)

    state = state.reshape(species, rows, lanes)
    inverse = inverse.reshape(species, species, rows, lanes)
    rates = jnp.pad(rates, ((0, padded - species),) * 2)

    def total(part):
        return lax.all_to_all(part, AXES, 0, 0)

    packed = call(pack_kernel, faces, [VMEM], (state,), cost=1 << 20, name="pack")
    xs, others = exchange(state, *packed)
    n = len(xs)
    rate0, base, weights, update, part = call(
        functools.partial(first_kernel, n),
        [block, block, block, block, partial],
        [VMEM] * (n + 5) + [SMEM, SMEM, VMEM, VMEM],
        (state, *xs, *others, diffusivity, boundary, rates, inverse),
        [flat, flat, edges],
        cost=8 << 20,
        name="first",
    )
    newton = functools.partial(next_kernel, entries)

    def iterate(part, base, update):
        return call(
            newton,
            [block, block, partial],
            [VMEM] * 6,
            (total(part), base, update, weights, rates, inverse),
            [flat, flat],
            cost=8 << 20,
            name="newton",
        )

    for _ in range(NEWTON - 1):
        base, update, part = iterate(part, base, update)
    section, *packed = call(
        functools.partial(section_kernel, entries),
        [block] + faces,
        [VMEM] * 3,
        (total(part), base, update),
        cost=1 << 20,
        name="section",
    )
    xs, others = exchange(section, *packed)
    base, update, part = call(
        functools.partial(second_kernel, n),
        [block, block, partial],
        [VMEM] * (n + 5) + [SMEM, SMEM] + [VMEM] * 5,
        (section, *xs, *others, diffusivity, boundary, rates, inverse, state, rate0, weights),
        [flat, flat, edges],
        cost=8 << 20,
        name="second",
    )
    for _ in range(NEWTON - 1):
        base, update, part = iterate(part, base, update)
    out = call(
        functools.partial(last_kernel, entries), block, [VMEM] * 3, (total(part), base, update), cost=1 << 19, name="last"
    )
    return out.reshape(species, nx, ny, lanes)


def solution(mesh):
    in_specs = (P(None, "gx", "gy", "gz"), P(), P(), P(None, None, "gx", "gy", "gz"), P())
    out_specs = P(None, "gx", "gy", "gz")
    return jax.shard_map(body, mesh=mesh, in_specs=in_specs, out_specs=out_specs, check_vma=False)
```

time: 228 us -> 94.9 us (0.42)
  other arithmetic: 54.5 us -> 0 us
  blocking collectives: 87.7 us -> 39.8 us
  waiting for transfers between devices: 36.9 us -> 7.98 us
  Pallas kernels: 0 us -> 20.3 us
  local copies, waits for them, and re-layouts: 23.7 us -> 11.7 us
  between operations: 5.08 us -> 0.05 us
  matrix products: 4.64 us -> 0 us
    psum x12 -> x0, blocking collectives: 87.7 us -> none  [the longest x4 39.5 us: global_total(): partial_z = lax.psum(local, 'gz')]
    unnamed x4 -> x0, other arithmetic: 40.2 us -> none
    all_to_all x0 -> x4, blocking collectives: none -> 39.8 us  [total(): return lax.all_to_all(part, AXES, 0, 0)]
    ppermute x12 -> x10, waiting for transfers between devices: 36.9 us -> 7.98 us  [the longest x2 5.47 us: exchange(): xs = [lax.ppermute(block, 'gx', ring('gx', 1))]]
    pallas_call x0 -> x7, Pallas kernels: none -> 20.3 us  [call(): pl.pallas_call(kernel, out_shape=outs, in_specs=specs, out_specs=jax.tree...]
    slice x23 -> x0, local copies, waits for them, and re-layouts: 14.5 us -> none  [the longest x7 9.46 us: with_halo(): lax.slice_in_dim(cells, cells.shape[dim] - width, cells.shape[dim], axis=...]
    select_n x11 -> x0, other arithmetic: 8.7 us -> none  [the longest x6 5.02 us: mirror_walls(): jnp.where(walled & (position == last_index), high_edge, high_ghost)]
    unnamed x40 -> x18, local copies, waits for them, and re-layouts: 5.26 us -> 10.9 us
  transfers between devices with their start and end apart: 12 -> 10, of which waited for: 9 -> 4; matrix products, arithmetic and copies ran while one was open for 6% -> 1% of each run, Pallas kernels for 0% -> 0%
where the time goes in v1:
time: 94.9 us; the launch traced here: 94.6 us
  blocking collectives  39.8 us (42%)
  Pallas kernels  20.3 us (21%)
  starting transfers between devices  14.8 us (16%)
  local copies, waits for them, and re-layouts  11.7 us (12%)
  waiting for transfers between devices  7.98 us (8%)
    all_to_all x4, blocking collectives, total(): return lax.all_to_all(part, AXES, 0, 0)  39.8 us
    pallas_call x7, Pallas kernels, call(): pl.pallas_call(kernel, out_shape=outs, in_specs=specs, out_specs=jax.tree...  20.3 us
    unnamed x18, local copies, waits for them, and re-layouts  10.9 us
    ppermute x2, starting transfers between devices, exchange(): lax.ppermute(head_z, 'gz', ring('gz', -1))  5.58 us
    ppermute x2, waiting for transfers between devices, exchange(): xs = [lax.ppermute(block, 'gx', ring('gx', 1))]  5.47 us
    ppermute x2, starting transfers between devices, exchange(): xs = [lax.ppermute(block, 'gx', ring('gx', 1))]  3.62 us
    ppermute x2, starting transfers between devices, exchange(): lax.ppermute(head_y, 'gy', ring('gy', -1))  3.48 us
    ppermute x2, waiting for transfers between devices, exchange(): lax.ppermute(tail_z, 'gz', ring('gz', 1))  2.49 us
  transfers between devices with their start and end apart: 10, of which 4 were waited for; matrix products, arithmetic and copies ran while one was open for 1% of the time, Pallas kernels for 0%

profile of v1, /device:TPU:0, one launch (start us, length us, event | category | flops | bytes accessed | tf_op | source)
XLA Modules:
  0.0 94.6 jit_solution(955285257124962019)
XLA Ops:
  0.0 3.0 %collective-permute-start = (f32[53,16,128]{2,1,0:T(8,128)}, f32[53,16,128]{2,1,0:T(8,128)S(1)}, u32[]{:S(2)}, u32[]{:S(2)}) collective-permute-start(f32[53,16,128]{2,1,0:T(8,128)} %bitcast.23), channel_id=1, source_target_pairs={{0,16},{16,0},{1,17},{17,1},{2,18},{18,2},{3,19},{19,3},{4,20},{20... | collective-permute-start | bytes 1302536 | tf_op jit(solution)/shard_map/ppermute | solution.py:310
  3.0 0.0 copy-start.2
  3.0 1.0 %copy-done.2 = f32[53,4,4,128]{3,2,1,0:T(4,128)S(1)} copy-done((f32[53,4,4,128]{3,2,1,0:T(4,128)S(1)}, f32[53,4,4,128]{3,2,1,0:T(4,128)}, u32[]{:S(2)}) %copy-start.2) | copy-done | bytes 434200
  4.0 0.3 pack.1
  4.3 0.1 collective-permute-start.1
  4.4 1.7 %collective-permute-start.2 = (f32[53,8,128]{2,1,0:T(8,128)S(1)}, f32[53,8,128]{2,1,0:T(8,128)S(1)}, u32[]{:S(2)}, u32[]{:S(2)}) collective-permute-start(f32[53,8,128]{2,1,0:T(8,128)S(1)} %get-tuple-element.29), channel_id=1, source_target_pairs={{0,12},{4,0},{8,4},{12,8},{1,13},{5,1},{9,5},{13,9},{2,14},{6,2},{... | collective-permute-start | bytes 651272 | tf_op jit(solution)/shard_map/ppermute | solution.py:314
  6.1 1.6 %collective-permute-start.3 = (f32[16,128]{1,0:T(8,128)S(1)}, f32[16,128]{1,0:T(8,128)S(1)}, u32[]{:S(2)}, u32[]{:S(2)}) collective-permute-start(f32[16,128]{1,0:T(8,128)S(1)} %get-tuple-element.30), channel_id=1, source_target_pairs={{0,1},{1,2},{2,3},{3,0},{4,5},{5,6},{6,7},{7,4},{8,9},{9,10},{10,1... | collective-permute-start | bytes 24584 | tf_op jit(solution)/shard_map/ppermute | solution.py:315
  7.7 2.2 %collective-permute-start.4 = (f32[16,128]{1,0:T(8,128)S(1)}, f32[16,128]{1,0:T(8,128)S(1)}, u32[]{:S(2)}, u32[]{:S(2)}) collective-permute-start(f32[16,128]{1,0:T(8,128)S(1)} %get-tuple-element.31), channel_id=1, source_target_pairs={{0,3},{1,0},{2,1},{3,2},{4,7},{5,4},{6,5},{7,6},{8,11},{9,8},{10,9... | collective-permute-start | bytes 24584 | tf_op jit(solution)/shard_map/ppermute | solution.py:315
  9.9 0.8 pad.4.refs_7_.rates
  10.7 0.9 collective-permute-done.3.refs_3_
  11.5 0.0 collective-permute-done.4.refs_4_
  11.5 0.0 collective-permute-done.1.refs_1_
  11.6 0.0 collective-permute-done.2.refs_2_
  11.6 1.6 %collective-permute-done.refs_0_ = f32[53,16,128]{2,1,0:T(8,128)S(1)} collective-permute-done((f32[53,16,128]{2,1,0:T(8,128)}, f32[53,16,128]{2,1,0:T(8,128)S(1)}, u32[]{:S(2)}, u32[]{:S(2)}) %collective-permute-start) | collective-permute-done | bytes 434208 | tf_op jit(solution)/shard_map/ppermute | solution.py:310
  13.2 0.0 copy-start
  13.2 7.5 %copy-done = f32[53,53,4,4,128]{4,3,2,1,0:T(4,128)S(1)} copy-done((f32[53,53,4,4,128]{4,3,2,1,0:T(4,128)S(1)}, f32[53,53,4,4,128]{4,3,2,1,0:T(4,128)}, u32[]{:S(2)}) %copy-start) | copy-done | bytes 23011352
  20.7 0.0 copy-start.3
  20.7 1.0 %copy-done.3 = f32[53,4,4,128]{3,2,1,0:T(4,128)S(1)} copy-done((f32[53,4,4,128]{3,2,1,0:T(4,128)S(1)}, f32[53,4,4,128]{3,2,1,0:T(4,128)}, u32[]{:S(2)}) %copy-start.3) | copy-done | bytes 434200
  21.7 0.0 copy-start.5
  21.7 0.7 copy-done.5
  22.4 0.0 copy-start.7
  22.4 0.7 copy-done.7
  23.0 0.0 copy-start.1
  23.0 0.0 copy-start.4
  23.0 0.0 copy-start.6
  23.0 0.0 copy-start.8
  23.0 5.2 %first.1 = (f32[53,16,128]{2,1,0:T(8,128)S(1)}, f32[53,16,128]{2,1,0:T(8,128)S(1)}, f32[53,16,128]{2,1,0:T(8,128)S(1)}, f32[53,16,128]{2,1,0:T(8,128)S(1)}, f32[32,128]{1,0:T(8,128)S(1)}) custom-call(f32[53,16,128]{2,1,0:T(8,128)S(1)} %bitcast.25, f32[53,16,128]{2,1,0:T(8,128)S(1)} %collective-permute-done.refs_0_, ...), custom_call_target="tpu_custom_call" | custom-call | flops 8388608 | bytes 8388608 | tf_op jit(solution)/shard_map/first/pallas_call | solution.py:290
  28.2 13.1 %all_to_all.44 = f32[32,1,128]{2,1,0:T(1,128)S(1)} all-to-all(f32[32,1,128]{2,1,0:T(1,128)S(1)} %bitcast.31), channel_id=1, replica_groups=mesh['gx'=2,'gy'=4,'gz'=4] {'gx','gy','gz'}, dimensions={0} | all-to-all | bytes 32768 | tf_op jit(solution)/shard_map/all_to_all | solution.py:339
  41.3 0.0 copy-done.1
  41.3 3.9 %newton.2 = (f32[53,16,128]{2,1,0:T(8,128)S(1)}, f32[53,16,128]{2,1,0:T(8,128)S(1)}, f32[32,128]{1,0:T(8,128)S(1)}) custom-call(f32[32,128]{1,0:T(8,128)S(1)} %bitcast.29, f32[53,16,128]{2,1,0:T(8,128)S(1)} %get-tuple-element.33.base, f32[53,16,128]{2,1,0:T(8,128)S(1)} %get-tuple-element.34.update, f32[53,16,128]{2,1,0:T(8,128)S(1)} %get-tuple-element.35.weights.refs_11_, ...), custom_call_target="tpu_custom_call" | custom-call | flops 8388608 | bytes 8388608 | tf_op jit(solution)/shard_map/newton/pallas_call | solution.py:290
  45.3 8.9 %all_to_all.45 = f32[32,1,128]{2,1,0:T(1,128)S(1)} all-to-all(f32[32,1,128]{2,1,0:T(1,128)S(1)} %bitcast.34), channel_id=1, replica_groups=mesh['gx'=2,'gy'=4,'gz'=4] {'gx','gy','gz'}, dimensions={0} | all-to-all | bytes 32768 | tf_op jit(solution)/shard_map/all_to_all | solution.py:339
  54.2 0.4 section.1
  54.6 0.7 collective-permute-start.5
  55.3 0.0 collective-permute-start.6
  55.3 1.7 %collective-permute-start.7 = (f32[53,8,128]{2,1,0:T(8,128)S(1)}, f32[53,8,128]{2,1,0:T(8,128)S(1)}, u32[]{:S(2)}, u32[]{:S(2)}) collective-permute-start(f32[53,8,128]{2,1,0:T(8,128)S(1)} %get-tuple-element.41), channel_id=1, source_target_pairs={{0,12},{4,0},{8,4},{12,8},{1,13},{5,1},{9,5},{13,9},{2,14},{6,2},{... | collective-permute-start | bytes 651272 | tf_op jit(solution)/shard_map/ppermute | solution.py:314
  57.0 0.5 collective-permute-start.8
  57.5 3.3 %collective-permute-start.9 = (f32[16,128]{1,0:T(8,128)S(1)}, f32[16,128]{1,0:T(8,128)S(1)}, u32[]{:S(2)}, u32[]{:S(2)}) collective-permute-start(f32[16,128]{1,0:T(8,128)S(1)} %get-tuple-element.43), channel_id=1, source_target_pairs={{0,3},{1,0},{2,1},{3,2},{4,7},{5,4},{6,5},{7,6},{8,11},{9,8},{10,9... | collective-permute-start | bytes 24584 | tf_op jit(solution)/shard_map/ppermute | solution.py:315
  60.8 1.6 %collective-permute-done.8.refs_3_ = f32[16,128]{1,0:T(8,128)S(1)} collective-permute-done((f32[16,128]{1,0:T(8,128)S(1)}, f32[16,128]{1,0:T(8,128)S(1)}, u32[]{:S(2)}, u32[]{:S(2)}) %collective-permute-start.8) | collective-permute-done | bytes 8224 | tf_op jit(solution)/shard_map/ppermute | solution.py:315
  62.5 0.0 collective-permute-done.9.refs_4_
  62.5 0.0 collective-permute-done.6.refs_1_
  62.5 0.0 collective-permute-done.7.refs_2_
  62.5 3.9 %collective-permute-done.5.refs_0_ = f32[53,16,128]{2,1,0:T(8,128)S(1)} collective-permute-done((f32[53,16,128]{2,1,0:T(8,128)S(1)}, f32[53,16,128]{2,1,0:T(8,128)S(1)}, u32[]{:S(2)}, u32[]{:S(2)}) %collective-permute-start.5) | collective-permute-done | bytes 434208 | tf_op jit(solution)/shard_map/ppermute | solution.py:310
  66.3 0.0 copy-done.4
  66.4 0.0 copy-done.6
  66.4 0.0 copy-done.8
  66.4 5.5 %second.1 = (f32[53,16,128]{2,1,0:T(8,128)S(1)}, f32[53,16,128]{2,1,0:T(8,128)S(1)}, f32[32,128]{1,0:T(8,128)S(1)}) custom-call(f32[53,16,128]{2,1,0:T(8,128)S(1)} %get-tuple-element.39.section, f32[53,16,128]{2,1,0:T(8,128)S(1)} %collective-permute-done.5.refs_0_, f32[53,8,128]{2,1,0:T(8,128)S(1)} %collective-permute-done.6.refs_1_, ...), custom_call_target="tpu_custom_call" | custom-call | flops 8388608 | bytes 8388608 | tf_op jit(solution)/shard_map/second/pallas_call | solution.py:290
  71.9 8.9 %all_to_all.46 = f32[32,1,128]{2,1,0:T(1,128)S(1)} all-to-all(f32[32,1,128]{2,1,0:T(1,128)S(1)} %bitcast.32), channel_id=1, replica_groups=mesh['gx'=2,'gy'=4,'gz'=4] {'gx','gy','gz'}, dimensions={0} | all-to-all | bytes 32768 | tf_op jit(solution)/shard_map/all_to_all | solution.py:339
  80.8 3.9 %newton.3 = (f32[53,16,128]{2,1,0:T(8,128)S(1)}, f32[53,16,128]{2,1,0:T(8,128)S(1)}, f32[32,128]{1,0:T(8,128)S(1)}) custom-call(f32[32,128]{1,0:T(8,128)S(1)} %bitcast.28, f32[53,16,128]{2,1,0:T(8,128)S(1)} %get-tuple-element.46.base, f32[53,16,128]{2,1,0:T(8,128)S(1)} %get-tuple-element.47.update, f32[53,16,128]{2,1,0:T(8,128)S(1)} %get-tuple-element.35.weights.refs_11_, ...), custom_call_target="tpu_custom_call" | custom-call | flops 8388608 | bytes 8388608 | tf_op jit(solution)/shard_map/newton/pallas_call | solution.py:290
  84.7 8.9 %all_to_all.47 = f32[32,1,128]{2,1,0:T(1,128)S(1)} all-to-all(f32[32,1,128]{2,1,0:T(1,128)S(1)} %bitcast.33), channel_id=1, replica_groups=mesh['gx'=2,'gy'=4,'gz'=4] {'gx','gy','gz'}, dimensions={0} | all-to-all | bytes 32768 | tf_op jit(solution)/shard_map/all_to_all | solution.py:339
  93.6 0.9 last.1
Async XLA Ops:
  0.0 13.2 %collective-permute-start = (f32[53,16,128]{2,1,0:T(8,128)}, f32[53,16,128]{2,1,0:T(8,128)S(1)}, u32[]{:S(2)}, u32[]{:S(2)}) collective-permute-start(f32[53,16,128]{2,1,0:T(8,128)} %bitcast.23), channel_id=1, source_target_pairs={{0,16},{16,0},{1,17},{17,1},{2,18},{18,2},{3,19},{19,3},{4,20},{20... | collective-permute-start | bytes 1302536 | tf_op jit(solution)/shard_map/ppermute | solution.py:310
  3.0 1.0 %copy-start.2 = (f32[53,4,4,128]{3,2,1,0:T(4,128)S(1)}, f32[53,4,4,128]{3,2,1,0:T(4,128)}, u32[]{:S(2)}) copy-start(f32[53,4,4,128]{3,2,1,0:T(4,128)} %param.5) | copy-start | bytes 1302532
  4.3 7.3 %collective-permute-start.1 = (f32[53,8,128]{2,1,0:T(8,128)S(1)}, f32[53,8,128]{2,1,0:T(8,128)S(1)}, u32[]{:S(2)}, u32[]{:S(2)}) collective-permute-start(f32[53,8,128]{2,1,0:T(8,128)S(1)} %get-tuple-element.28), channel_id=1, source_target_pairs={{0,4},{4,8},{8,12},{12,0},{1,5},{5,9},{9,13},{13,1},{2,6},{6,10},{... | collective-permute-start | bytes 651272 | tf_op jit(solution)/shard_map/ppermute | solution.py:314
  4.4 7.2 %collective-permute-start.2 = (f32[53,8,128]{2,1,0:T(8,128)S(1)}, f32[53,8,128]{2,1,0:T(8,128)S(1)}, u32[]{:S(2)}, u32[]{:S(2)}) collective-permute-start(f32[53,8,128]{2,1,0:T(8,128)S(1)} %get-tuple-element.29), channel_id=1, source_target_pairs={{0,12},{4,0},{8,4},{12,8},{1,13},{5,1},{9,5},{13,9},{2,14},{6,2},{... | collective-permute-start | bytes 651272 | tf_op jit(solution)/shard_map/ppermute | solution.py:314
  6.1 5.4 %collective-permute-start.3 = (f32[16,128]{1,0:T(8,128)S(1)}, f32[16,128]{1,0:T(8,128)S(1)}, u32[]{:S(2)}, u32[]{:S(2)}) collective-permute-start(f32[16,128]{1,0:T(8,128)S(1)} %get-tuple-element.30), channel_id=1, source_target_pairs={{0,1},{1,2},{2,3},{3,0},{4,5},{5,6},{6,7},{7,4},{8,9},{9,10},{10,1... | collective-permute-start | bytes 24584 | tf_op jit(solution)/shard_map/ppermute | solution.py:315
  7.7 3.9 %collective-permute-start.4 = (f32[16,128]{1,0:T(8,128)S(1)}, f32[16,128]{1,0:T(8,128)S(1)}, u32[]{:S(2)}, u32[]{:S(2)}) collective-permute-start(f32[16,128]{1,0:T(8,128)S(1)} %get-tuple-element.31), channel_id=1, source_target_pairs={{0,3},{1,0},{2,1},{3,2},{4,7},{5,4},{6,5},{7,6},{8,11},{9,8},{10,9... | collective-permute-start | bytes 24584 | tf_op jit(solution)/shard_map/ppermute | solution.py:315
  13.2 7.5 %copy-start = (f32[53,53,4,4,128]{4,3,2,1,0:T(4,128)S(1)}, f32[53,53,4,4,128]{4,3,2,1,0:T(4,128)}, u32[]{:S(2)}) copy-start(f32[53,53,4,4,128]{4,3,2,1,0:T(4,128)} %param.8) | copy-start | bytes 69033984
  20.7 1.0 %copy-start.3 = (f32[53,4,4,128]{3,2,1,0:T(4,128)S(1)}, f32[53,4,4,128]{3,2,1,0:T(4,128)}, u32[]{:S(2)}) copy-start(f32[53,4,4,128]{3,2,1,0:T(4,128)} %param.5) | copy-start | bytes 1302532
  21.7 0.7 copy-start.5
  22.4 0.7 copy-start.7
  23.0 18.3 %copy-start.1 = (f32[53,53,4,4,128]{4,3,2,1,0:T(4,128)S(1)}, f32[53,53,4,4,128]{4,3,2,1,0:T(4,128)}, u32[]{:S(2)}) copy-start(f32[53,53,4,4,128]{4,3,2,1,0:T(4,128)} %param.8) | copy-start | bytes 69033984
  23.0 43.3 %copy-start.4 = (f32[53,4,4,128]{3,2,1,0:T(4,128)S(1)}, f32[53,4,4,128]{3,2,1,0:T(4,128)}, u32[]{:S(2)}) copy-start(f32[53,4,4,128]{3,2,1,0:T(4,128)} %param.5) | copy-start | bytes 1302532
  23.0 43.3 %copy-start.6 = (f32[53]{0:T(128)S(1)}, f32[53]{0:T(128)}, u32[]{:S(2)}) copy-start(f32[53]{0:T(128)} %refs_5_.3) | copy-start | bytes 640
  23.0 43.3 %copy-start.8 = (s32[3]{0:T(128)S(1)}, s32[3]{0:T(128)}, u32[]{:S(2)}) copy-start(s32[3]{0:T(128)} %refs_6_.3) | copy-start | bytes 40
  54.6 11.7 %collective-permute-start.5 = (f32[53,16,128]{2,1,0:T(8,128)S(1)}, f32[53,16,128]{2,1,0:T(8,128)S(1)}, u32[]{:S(2)}, u32[]{:S(2)}) collective-permute-start(f32[53,16,128]{2,1,0:T(8,128)S(1)} %get-tuple-element.39.section), channel_id=1, source_target_pairs={{0,16},{16,0},{1,17},{17,1},{2,18},{18,2},{3,19},{19,3},{4,20},{20... | collective-permute-start | bytes 1302536 | tf_op jit(solution)/shard_map/ppermute | solution.py:310
  55.3 7.2 %collective-permute-start.6 = (f32[53,8,128]{2,1,0:T(8,128)S(1)}, f32[53,8,128]{2,1,0:T(8,128)S(1)}, u32[]{:S(2)}, u32[]{:S(2)}) collective-permute-start(f32[53,8,128]{2,1,0:T(8,128)S(1)} %get-tuple-element.40), channel_id=1, source_target_pairs={{0,4},{4,8},{8,12},{12,0},{1,5},{5,9},{9,13},{13,1},{2,6},{6,10},{... | collective-permute-start | bytes 651272 | tf_op jit(solution)/shard_map/ppermute | solution.py:314
  55.3 7.2 %collective-permute-start.7 = (f32[53,8,128]{2,1,0:T(8,128)S(1)}, f32[53,8,128]{2,1,0:T(8,128)S(1)}, u32[]{:S(2)}, u32[]{:S(2)}) collective-permute-start(f32[53,8,128]{2,1,0:T(8,128)S(1)} %get-tuple-element.41), channel_id=1, source_target_pairs={{0,12},{4,0},{8,4},{12,8},{1,13},{5,1},{9,5},{13,9},{2,14},{6,2},{... | collective-permute-start | bytes 651272 | tf_op jit(solution)/shard_map/ppermute | solution.py:314
  57.0 5.4 %collective-permute-start.8 = (f32[16,128]{1,0:T(8,128)S(1)}, f32[16,128]{1,0:T(8,128)S(1)}, u32[]{:S(2)}, u32[]{:S(2)}) collective-permute-start(f32[16,128]{1,0:T(8,128)S(1)} %get-tuple-element.42), channel_id=1, source_target_pairs={{0,1},{1,2},{2,3},{3,0},{4,5},{5,6},{6,7},{7,4},{8,9},{9,10},{10,1... | collective-permute-start | bytes 24584 | tf_op jit(solution)/shard_map/ppermute | solution.py:315
  57.5 5.0 %collective-permute-start.9 = (f32[16,128]{1,0:T(8,128)S(1)}, f32[16,128]{1,0:T(8,128)S(1)}, u32[]{:S(2)}, u32[]{:S(2)}) collective-permute-start(f32[16,128]{1,0:T(8,128)S(1)} %get-tuple-element.43), channel_id=1, source_target_pairs={{0,3},{1,0},{2,1},{3,2},{4,7},{5,4},{6,5},{7,6},{8,11},{9,8},{10,9... | collective-permute-start | bytes 24584 | tf_op jit(solution)/shard_map/ppermute | solution.py:315
